TPU v7x, 32 devices: a whole 2x2x4 slice. The times are simulated.
32 devices in a mesh: img: 4 (over x, core), slab: 8 (over z, y).
Axes of the slice: x: 2, y: 2, z: 4, core: 2. Of those that a mesh axis runs over, the one named last changes fastest.
Arguments:
- section_input: bfloat16 [256, 256, 1024], P(('img', 'slab')), parts along dimension 0, may hold values from -54 to 54
- w_reduce: bfloat16 [3, 1024, 256], replicated, may hold values from -0.1875 to 0.1875
- w_spatial: bfloat16 [3, 9, 256, 256], replicated, may hold values from -0.125 to 0.125
- w_expand: bfloat16 [3, 256, 1024], replicated, may hold values from -0.375 to 0.375
- gain_mid: float32 [3, 2, 256], replicated, may hold values from 0.25 to 1.75
- shift_mid: float32 [3, 2, 256], replicated, may hold values from -3 to 3
- gain_out: float32 [3, 1024], replicated, may hold values from 0.25 to 1.75
- shift_out: float32 [3, 1024], replicated, may hold values from -3 to 3
Outputs:
- section_output: bfloat16 [256, 256, 1024], P(('img', 'slab')), parts along dimension 0
There are 4 independent parts, one for each index of `img`. A program takes and returns all parts, laid end to end along the dimension named above; an argument that names none is the same for every part. Nothing has to cross between parts.
All inputs are finite; a program needn't handle non-finite values.
Results may differ from a plain program's by a relative error of at most 0.01.
Values may be sent and summed in bfloat16 or wider, within the bound.
A program may use at most 128 MiB of HBM per device.

v0:
```python
import functools

import jax
import jax.numpy as jnp
from jax import lax
from jax.experimental import pallas as pl
from jax.experimental.pallas import tpu as pltpu
from jax.sharding import PartitionSpec as P

MESH = pl.DeviceIdType.MESH
EPS = 1e-05
REDUCE_ROWS = 2
CONV_ROWS = 6
EXPAND_ROWS = 8
OUTPUT_ROWS = 4


def divisor(rows, most):
    return max(d for d in range(1, most + 1) if rows % d == 0)


def kernel(
    n, x_hbm, wr_hbm, ws_hbm, we_hbm, gain_mid, shift_mid, gain_out, shift_out, out_hbm,
    x, wr, ws, we, red, taps, inner, expanded, halo_out, halo_in, stat_out, stat, sums,
    x_sem, w_sem, out_sem, halo_send, halo_recv, stat_send, stat_recv,
):
    rows, width, chans = x.shape
    layers, _, mid = wr.shape
    chunks = chans // mid
    stages = 2 + chunks
    reduce_rows = divisor(rows, REDUCE_ROWS)
    conv_rows = divisor(rows - 2, CONV_ROWS)
    expand_rows = divisor(rows, EXPAND_ROWS)
    output_rows = divisor(rows, OUTPUT_ROWS)
    me = lax.axis_index("slab")
    inv_local = 1.0 / (rows * width)
    inv_count = 1.0 / (rows * width * n)

    def peer(k):
        return lax.rem(me + k, n)

    barrier = pltpu.get_barrier_semaphore()
    for k in range(1, n):
        pl.semaphore_signal(barrier, inc=1, device_id={"slab": peer(k)}, device_id_type=MESH)

    def weight_copy(kind, layer):
        source, target = ((wr_hbm, wr), (ws_hbm, ws), (we_hbm, we))[kind]
        return pltpu.make_async_copy(source.at[layer], target.at[layer], w_sem.at[kind, layer])

    def x_copy(row):
        return pltpu.make_async_copy(x_hbm.at[row], x.at[row], x_sem.at[row])

    def out_copy(chunk):
        cols = pl.ds(chunk * mid, mid)
        return pltpu.make_async_copy(x.at[:, :, cols], out_hbm.at[:, :, cols], out_sem.at[chunk])

    weight_copy(0, 0).start()
    for row in range(rows):
        x_copy(row).start()

    def stat_copy(stage, k):
        return pltpu.make_async_remote_copy(
            src_ref=stat_out.at[stage],
            dst_ref=stat.at[stage, me],
            send_sem=stat_send.at[stage, k],
            recv_sem=stat_recv.at[stage, me],
            device_id={"slab": peer(k)},
            device_id_type=MESH,
        )

    def stat_arrival(stage, k):
        source = peer(k)
        return pltpu.make_async_remote_copy(
            src_ref=stat_out.at[stage],
            dst_ref=stat.at[stage, source],
            send_sem=stat_send.at[stage, k],
            recv_sem=stat_recv.at[stage, source],
            device_id={"slab": source},
            device_id_type=MESH,
        )

    def fold(carry, y):
        total, squares = carry
        y = y.reshape(-1, 8, mid)
        return total + jnp.sum(y, axis=0), squares + jnp.sum(y * y, axis=0)

    def zeros():
        return jnp.zeros((8, mid), jnp.float32), jnp.zeros((8, mid), jnp.float32)

    def send_stats(stage, carry):
        total = jnp.sum(carry[0], axis=0, keepdims=True)
        squares = jnp.sum(carry[1], axis=0, keepdims=True)
        both = jnp.concatenate([total, squares], axis=0)
        stat_out[stage] = both
        stat[stage, me] = both
        for k in range(1, n):
            stat_copy(stage, k).start()
        return total

    def affine(stage, gain, shift):
        for k in range(1, n):
            stat_copy(stage, k).wait_send()
            stat_arrival(stage, k).wait_recv()
        both = jnp.sum(stat[stage], axis=0)
        mean = both[0:1] * inv_count
        var = jnp.maximum(both[1:2] * inv_count - mean * mean, 0.0)
        scale = lax.rsqrt(var + EPS) * gain
        return scale, shift - mean * scale

    def halo_copy(layer, side):
        return pltpu.make_async_remote_copy(
            src_ref=halo_out.at[layer, side],
            dst_ref=halo_in.at[layer, 1 - side],
            send_sem=halo_send.at[layer, side],
            recv_sem=halo_recv.at[layer, 1 - side],
            device_id={"slab": peer(n - 1 if side == 0 else 1)},
            device_id_type=MESH,
        )

    def halo_arrival(layer, side):
        return pltpu.make_async_remote_copy(
            src_ref=halo_out.at[layer, side],
            dst_ref=halo_in.at[layer, side],
            send_sem=halo_send.at[layer, side],
            recv_sem=halo_recv.at[layer, side],
            device_id={"slab": peer(n - 1 if side == 0 else 1)},
            device_id_type=MESH,
        )

    def has_neighbour(side):
        return me > 0 if side == 0 else me < n - 1

    column = lax.broadcasted_iota(jnp.int32, (width, mid), 0)

    def store_taps(row, h):
        at = pl.ds(row * width, width)
        before = jnp.where(column == 0, 0.0, pltpu.roll(h, 1, 0))
        after = jnp.where(column == width - 1, 0.0, pltpu.roll(h, width - 1, 0))
        taps[at, 0:mid] = before.astype(jnp.bfloat16)
        taps[at, mid : 2 * mid] = h.astype(jnp.bfloat16)
        taps[at, 2 * mid : 3 * mid] = after.astype(jnp.bfloat16)

    def keep_sums(carry):
        sums[0] = carry[0]
        sums[1] = carry[1]

    def reduce_step(i, carry):
        for r in range(reduce_rows):
            x_copy(i * reduce_rows + r).wait()
        y = jnp.dot(
            x[pl.ds(i * reduce_rows, reduce_rows)].reshape(reduce_rows * width, chans),
            wr[0],
            preferred_element_type=jnp.float32,
        )
        red[pl.ds(i * reduce_rows * width, reduce_rows * width), :] = y
        return fold(carry, y)

    weight_copy(0, 0).wait()
    keep_sums(lax.fori_loop(0, rows // reduce_rows, reduce_step, zeros()))
    pl.semaphore_wait(barrier, n - 1)

    def layer_step(layer, _):
        first = layer * stages

        carry = (sums[0], sums[1])
        local_mean = send_stats(first, carry) * inv_local
        for side in range(2):
            row = 0 if side == 0 else rows - 1
            halo_out[layer, side] = (red[row * width : (row + 1) * width, :] - local_mean).astype(
                jnp.bfloat16
            )

            @pl.when(has_neighbour(side))
            def _():
                halo_copy(layer, side).start()

        weight_copy(1, layer).start()
        weight_copy(2, layer).start()

        @pl.when(layer < layers - 1)
        def _():
            weight_copy(0, layer + 1).start()

        scale, shift = affine(first, gain_mid[layer, 0:1], shift_mid[layer, 0:1])

        def hidden_step(i, _):
            y = red[pl.ds(i * width, width), :]
            store_taps(i + 1, jnp.maximum(y * scale + shift, 0.0))
            return 0

        lax.fori_loop(0, rows, hidden_step, 0)

        weight_copy(1, layer).wait()

        def conv(row, count):
            total = None
            for down in range(3):
                part = jnp.dot(
                    taps[pl.ds((row + down) * width, count * width), :],
                    ws[layer, pl.ds(3 * down, 3)].reshape(3 * mid, mid),
                    preferred_element_type=jnp.float32,
                )
                total = part if total is None else total + part
            red[pl.ds(row * width, count * width), :] = total
            return total

        def inside_step(i, carry):
            return fold(carry, conv(1 + i * conv_rows, conv_rows))

        carry = lax.fori_loop(0, (rows - 2) // conv_rows, inside_step, zeros())

        for side in range(2):
            source = peer(n - 1 if side == 0 else 1)
            row = 0 if side == 0 else rows + 1

            @pl.when(has_neighbour(side))
            def _():
                halo_copy(layer, side).wait_send()
                halo_arrival(layer, side).wait_recv()
                theirs = stat[first, source][0:1] * inv_local
                y = halo_in[layer, side].astype(jnp.float32) + theirs
                store_taps(row, jnp.maximum(y * scale + shift, 0.0))

            @pl.when(jnp.logical_not(has_neighbour(side)))
            def _():
                taps[pl.ds(row * width, width), :] = jnp.zeros((width, 3 * mid), jnp.bfloat16)

        def edge_step(i, carry):
            return fold(carry, conv(i * (rows - 1), 1))

        carry = lax.fori_loop(0, 2, edge_step, carry)
        send_stats(first + 1, carry)

        scale, shift = affine(first + 1, gain_mid[layer, 1:2], shift_mid[layer, 1:2])

        weight_copy(2, layer).wait()
        for c in range(chunks):
            cols = slice(c * mid, (c + 1) * mid)

            def expand_step(i, carry):
                at = pl.ds(i * expand_rows * width, expand_rows * width)
                if c == 0:
                    block = jnp.maximum(red[at, :] * scale + shift, 0.0).astype(jnp.bfloat16)
                    inner[at, :] = block
                else:
                    block = inner[at, :]
                y = jnp.dot(block, we[layer, :, cols], preferred_element_type=jnp.float32)
                expanded[c, at, :] = y
                return fold(carry, y)

            send_stats(first + 2 + c, lax.fori_loop(0, rows // expand_rows, expand_step, zeros()))

        @pl.when(layer < layers - 1)
        def _():
            weight_copy(0, layer + 1).wait()

        for c in range(chunks):
            cols = slice(c * mid, (c + 1) * mid)
            scale, shift = affine(
                first + 2 + c,
                gain_out[pl.ds(layer, 1), cols],
                shift_out[pl.ds(layer, 1), cols],
            )

            def output(row, count):
                at = pl.ds(row * width, count * width)
                y = expanded[c, at, :] * scale + shift
                y = y + x[pl.ds(row, count), :, cols].reshape(count * width, mid).astype(jnp.float32)
                y = jnp.maximum(y, 0.0).astype(jnp.bfloat16)
                x[pl.ds(row, count), :, cols] = y.reshape(count, width, mid)
                return y

            @pl.when(layer < layers - 1)
            def _():
                def output_step(i, carry):
                    at = pl.ds(i * output_rows * width, output_rows * width)
                    y = jnp.dot(
                        output(i * output_rows, output_rows),
                        wr[layer + 1, cols, :],
                        preferred_element_type=jnp.float32,
                    )
                    if c > 0:
                        y = y + red[at, :]
                    red[at, :] = y
                    return fold(carry, y) if c == chunks - 1 else carry

                if c == chunks - 1:
                    keep_sums(lax.fori_loop(0, rows // output_rows, output_step, zeros()))
                else:
                    lax.fori_loop(0, rows // output_rows, output_step, 0)

            @pl.when(layer == layers - 1)
            def _():
                def output_step(i, _):
                    output(i, 1)
                    return 0

                lax.fori_loop(0, rows, output_step, 0)
                out_copy(c).start()

        return 0

    lax.fori_loop(0, layers, layer_step, 0)
    for c in range(chunks):
        out_copy(c).wait()


def solution(mesh):
    n = mesh.shape["slab"]

    def local(section_input, w_reduce, w_spatial, w_expand, gain_mid, shift_mid, gain_out, shift_out):
        rows, width, chans = section_input.shape
        layers, _, mid = w_reduce.shape
        chunks = chans // mid
        total = layers * (2 + chunks)
        bf16, f32 = jnp.bfloat16, jnp.float32
        hbm = pl.BlockSpec(memory_space=pl.ANY)
        vmem = pl.BlockSpec(memory_space=pltpu.VMEM)
        return pl.pallas_call(
            functools.partial(kernel, n),
            out_shape=jax.ShapeDtypeStruct(section_input.shape, bf16),
            in_specs=[hbm] * 4 + [vmem] * 4,
            out_specs=hbm,
            scratch_shapes=[
                pltpu.VMEM((rows, width, chans), bf16),
                pltpu.VMEM(w_reduce.shape, bf16),
                pltpu.VMEM(w_spatial.shape, bf16),
                pltpu.VMEM(w_expand.shape, bf16),
                pltpu.VMEM((rows * width, mid), f32),
                pltpu.VMEM(((rows + 2) * width, 3 * mid), bf16),
                pltpu.VMEM((rows * width, mid), bf16),
                pltpu.VMEM((chunks, rows * width, mid), f32),
                pltpu.VMEM((layers, 2, width, mid), bf16),
                pltpu.VMEM((layers, 2, width, mid), bf16),
                pltpu.VMEM((total, 2, mid), f32),
                pltpu.VMEM((total, n, 2, mid), f32),
                pltpu.VMEM((2, 8, mid), f32),
                pltpu.SemaphoreType.DMA((rows,)),
                pltpu.SemaphoreType.DMA((3, layers)),
                pltpu.SemaphoreType.DMA((chunks,)),
                pltpu.SemaphoreType.DMA((layers, 2)),
                pltpu.SemaphoreType.DMA((layers, 2)),
                pltpu.SemaphoreType.DMA((total, n)),
                pltpu.SemaphoreType.DMA((total, n)),
            ],
            compiler_params=pltpu.CompilerParams(
                collective_id=0, has_side_effects=True, vmem_limit_bytes=56 * 1024 * 1024
            ),
            name="blocks",
        )(section_input, w_reduce, w_spatial, w_expand, gain_mid, shift_mid, gain_out, shift_out)

    placed = (P(("img", "slab"), None, None), P(), P(), P(), P(), P(), P(), P())
    return jax.shard_map(
        local, mesh=mesh, in_specs=placed, out_specs=P(("img", "slab"), None, None), check_vma=False
    )
```

profile of v0, /device:TPU:0, one launch (start us, length us, event | category | flops | bytes accessed | tf_op | source)
XLA Modules:
  0.0 75.9 jit_solution(1870778041020003890)
XLA Ops:
  0.0 71.3 %blocks.1 = bf16[8,256,1024]{2,1,0:T(8,128)(2,1)} custom-call(bf16[8,256,1024]{2,1,0:T(8,128)(2,1)} %x_hbm.1, bf16[3,1024,256]{2,1,0:T(8,128)(2,1)} %wr_hbm.1, bf16[3,9,256,256]{3,2,1,0:T(8,128)(2,1)} %ws_hbm.1, bf16[3,256,1024]{2,1,0:T(8,128)(2,1)} %we_hbm.1, f32[3,2,256]{2,1,0:T(2,128)} %gain_mid.1, f32[3,2,256]{2,1,0:T(2,128)} %shift_mid.1, ...), custom_call_target="tpu_custom_call" | custom-call | tf_op jit(solution)/shard_map/blocks/pallas_call | solution.py:319
  71.3 4.6 %copy.10 = bf16[8,256,1024]{2,1,0:T(8,128)(2,1)} copy(bf16[8,256,1024]{2,1,0:T(8,128)(2,1)} %blocks.1) | data formatting | bytes 8388608
where the time goes:
time: 76.2 us; the launch traced here: 75.9 us
  Pallas kernels  71.3 us (94%)
  local copies, waits for them, and re-layouts  4.64 us (6%)
    pallas_call x1, Pallas kernels, local(): pl.pallas_call(functools.partial(kernel, n), out_shape=jax.ShapeDtypeStru...  71.3 us
    unnamed x1, local copies, waits for them, and re-layouts  4.64 us

commit v1 on v0

v1 whole, which is shorter than its diff:
```python
import functools

import jax
import jax.numpy as jnp
from jax import lax
from jax.experimental import pallas as pl
from jax.experimental.pallas import tpu as pltpu
from jax.sharding import PartitionSpec as P

MESH = pl.DeviceIdType.MESH
EPS = 1e-05
REDUCE_ROWS = 2
CONV_ROWS = 2
EXPAND_ROWS = 1
OUTPUT_ROWS = 1
FINAL_ROWS = 1
LANES = 8
GROUP = 2


def divisor(rows, most):
    return max(d for d in range(1, most + 1) if rows % d == 0)


def kernel(
    n, x_hbm, wr_hbm, ws_hbm, we_hbm, gain_mid, shift_mid, gain_out, shift_out,
    expanded, x, last,
    wr, ws, we, red, taps, inner, halo_out, halo_in, stat_out, stat, sums,
    x_sem, w_sem, halo_send, halo_recv, stat_send, stat_recv,
):
    chunks, count, mid = x.shape
    rows, width, chans = x_hbm.shape
    layers = wr.shape[0]
    group = divisor(chunks, GROUP)
    groups = chunks // group
    wide = group * mid
    stages = 2 + groups
    me = lax.axis_index("slab")
    inv_local = 1.0 / count
    inv_count = 1.0 / (count * n)

    def peer(k):
        return lax.rem(me + k, n)

    barrier = pltpu.get_barrier_semaphore()
    for k in range(1, n):
        pl.semaphore_signal(barrier, inc=1, device_id={"slab": peer(k)}, device_id_type=MESH)

    def weight_copy(kind, layer):
        source, target = ((wr_hbm, wr), (ws_hbm, ws), (we_hbm, we))[kind]
        return pltpu.make_async_copy(source.at[layer], target.at[layer], w_sem.at[kind, layer])

    def x_copy(row, c):
        return pltpu.make_async_copy(
            x_hbm.at[row, :, pl.ds(c * mid, mid)],
            x.at[c, pl.ds(row * width, width), :],
            x_sem.at[row, c],
        )

    weight_copy(0, 0).start()
    for row in range(rows):
        for c in range(chunks):
            x_copy(row, c).start()

    def span(row, many=1):
        return pl.ds(row * width, many * width)

    def stat_copy(stage, cols, k):
        return pltpu.make_async_remote_copy(
            src_ref=stat_out.at[stage],
            dst_ref=stat.at[stage, k],
            send_sem=stat_send.at[stage],
            recv_sem=stat_recv.at[stage],
            device_id={"slab": peer(k)},
            device_id_type=MESH,
        )

    def all_stats(stage, sem):
        others = stat.at[stage, pl.ds(1, n - 1)]
        return pltpu.make_async_copy(others, others, sem.at[stage])

    def fold(carry, y):
        y = y.reshape(-1, LANES, 8, y.shape[-1])
        return carry[0] + jnp.sum(y, axis=0), carry[1] + jnp.sum(y * y, axis=0)

    def zeros(cols):
        zero = jnp.zeros((LANES, 8, cols), jnp.float32)
        return zero, zero

    def total(part):
        return jnp.sum(jnp.sum(part, axis=0), axis=0, keepdims=True)

    def send_stats(stage, carry):
        first = total(carry[0])
        both = jnp.concatenate([first, total(carry[1])], axis=0)
        cols = both.shape[-1]
        stat_out[stage, :, 0:cols] = both
        stat[stage, 0, :, 0:cols] = both
        for k in range(1, n):
            stat_copy(stage, cols, k).start()
        return first

    def affine(stage, gain, shift):
        all_stats(stage, stat_recv).wait()
        cols = gain.shape[-1]
        both = jnp.sum(stat[stage], axis=0)[:, 0:cols]
        mean = both[0:1] * inv_count
        var = jnp.maximum(both[1:2] * inv_count - mean * mean, 0.0)
        scale = lax.rsqrt(var + EPS) * gain
        return scale, shift - mean * scale

    def halo_copy(layer, side):
        return pltpu.make_async_remote_copy(
            src_ref=halo_out.at[layer, side],
            dst_ref=halo_in.at[layer, 1 - side],
            send_sem=halo_send.at[layer, side],
            recv_sem=halo_recv.at[layer, 1 - side],
            device_id={"slab": peer(n - 1 if side == 0 else 1)},
            device_id_type=MESH,
        )

    def halo_arrival(layer, side):
        return pltpu.make_async_remote_copy(
            src_ref=halo_out.at[layer, side],
            dst_ref=halo_in.at[layer, side],
            send_sem=halo_send.at[layer, side],
            recv_sem=halo_recv.at[layer, side],
            device_id={"slab": peer(n - 1 if side == 0 else 1)},
            device_id_type=MESH,
        )

    def has_neighbour(side):
        return me > 0 if side == 0 else me < n - 1

    edge = lax.broadcasted_iota(jnp.int32, (16, mid), 0)

    def store_taps(row, h):
        at = span(row)
        before = pltpu.roll(h, 1, 0)
        after = pltpu.roll(h, width - 1, 0)
        taps[at, mid : 2 * mid] = h.astype(jnp.bfloat16)
        before = jnp.concatenate([jnp.where(edge == 0, 0.0, before[0:16]), before[16:]], axis=0)
        taps[at, 0:mid] = before.astype(jnp.bfloat16)
        after = jnp.concatenate(
            [after[: width - 16], jnp.where(edge == 15, 0.0, after[width - 16 :])], axis=0
        )
        taps[at, 2 * mid : 3 * mid] = after.astype(jnp.bfloat16)

    def keep_sums(carry):
        sums[0] = carry[0]
        sums[1] = carry[1]

    for side in range(2):
        row = 0 if side == 0 else rows + 1
        taps[span(row), :] = jnp.zeros((width, 3 * mid), jnp.bfloat16)

    weight_copy(0, 0).wait()
    carry = zeros(mid)
    reduce_rows = divisor(rows, REDUCE_ROWS)
    for row in range(0, rows, reduce_rows):
        for r in range(row, row + reduce_rows):
            for c in range(chunks):
                x_copy(r, c).wait()
        for r in range(row, row + reduce_rows):
            y = jnp.dot(
                jnp.concatenate([x[c, span(r), :] for c in range(chunks)], axis=1),
                wr[0],
                preferred_element_type=jnp.float32,
            )
            red[span(r), :] = y
            carry = fold(carry, y)
    keep_sums(carry)
    pl.semaphore_wait(barrier, n - 1)

    def layer_step(layer, _):
        first = layer * stages

        local_mean = send_stats(first, (sums[0], sums[1])) * inv_local
        for side in range(2):
            row = 0 if side == 0 else rows - 1
            halo_out[layer, side] = (red[span(row), :] - local_mean).astype(jnp.bfloat16)

            @pl.when(has_neighbour(side))
            def _():
                halo_copy(layer, side).start()

        weight_copy(1, layer).start()
        weight_copy(2, layer).start()

        @pl.when(layer < layers - 1)
        def _():
            weight_copy(0, layer + 1).start()

        weight_copy(1, layer).wait()
        scale, shift = affine(first, gain_mid[layer, 0:1], shift_mid[layer, 0:1])

        def hidden(row):
            store_taps(row + 1, jnp.maximum(red[span(row), :] * scale + shift, 0.0))

        def conv(row, many):
            y = jnp.dot(
                jnp.concatenate([taps[span(row + down, many), :] for down in range(3)], axis=1),
                ws[layer].reshape(9 * mid, mid),
                preferred_element_type=jnp.float32,
            )
            red[span(row, many), :] = y
            return y

        carry = zeros(mid)
        done = 0
        conv_rows = divisor(rows - 2, CONV_ROWS)
        for row in range(1, rows - 1, conv_rows):
            while done < row + conv_rows + 1:
                hidden(done)
                done += 1
            for r in range(row, row + conv_rows):
                carry = fold(carry, conv(r, 1))

        for side in range(2):
            row = 0 if side == 0 else rows + 1

            @pl.when(has_neighbour(side))
            def _():
                halo_copy(layer, side).wait_send()
                halo_arrival(layer, side).wait_recv()
                theirs = stat[first, 1 if side == 0 else n - 1, 0:1, 0:mid] * inv_local
                y = halo_in[layer, side].astype(jnp.float32) + theirs
                store_taps(row, jnp.maximum(y * scale + shift, 0.0))

        for row in (0, rows - 1):
            carry = fold(carry, conv(row, 1))
        send_stats(first + 1, carry)

        weight_copy(2, layer).wait()
        scale, shift = affine(first + 1, gain_mid[layer, 1:2], shift_mid[layer, 1:2])

        expand_rows = divisor(rows, EXPAND_ROWS)
        for g in range(groups):
            parts = [zeros(mid) for _ in range(group)]
            for row in range(0, rows, expand_rows):
                at = span(row, expand_rows)
                if g == 0:
                    block = jnp.maximum(red[at, :] * scale + shift, 0.0).astype(jnp.bfloat16)
                    inner[at, :] = block
                else:
                    block = inner[at, :]
                for i in range(group):
                    c = g * group + i
                    y = jnp.dot(
                        block, we[layer, :, c * mid : (c + 1) * mid],
                        preferred_element_type=jnp.float32,
                    )
                    expanded[c, at, :] = y
                    parts[i] = fold(parts[i], y)
            send_stats(
                first + 2 + g,
                tuple(jnp.concatenate([p[j] for p in parts], axis=-1) for j in range(2)),
            )

        @pl.when(layer < layers - 1)
        def _():
            weight_copy(0, layer + 1).wait()

        output_rows = divisor(rows, OUTPUT_ROWS)
        carry = zeros(mid)
        for g in range(groups):
            cols = slice(g * wide, (g + 1) * wide)
            scale, shift = affine(
                first + 2 + g, gain_out[pl.ds(layer, 1), cols], shift_out[pl.ds(layer, 1), cols]
            )

            @pl.when(layer == layers - 1)
            def _():
                last[0:1, cols] = scale
                last[1:2, cols] = shift

            @pl.when(layer < layers - 1)
            def _():
                carry = zeros(mid)
                for row in range(0, rows, output_rows):
                    at = span(row, output_rows)
                    blocks = []
                    for i in range(group):
                        c = g * group + i
                        part = slice(i * mid, (i + 1) * mid)
                        y = expanded[c, at, :] * scale[:, part] + shift[:, part]
                        y = y + x[c, at, :].astype(jnp.float32)
                        y = jnp.maximum(y, 0.0).astype(jnp.bfloat16)
                        x[c, at, :] = y
                        blocks.append(y)
                    y = jnp.dot(
                        jnp.concatenate(blocks, axis=1),
                        wr[layer + 1, cols, :],
                        preferred_element_type=jnp.float32,
                    )
                    if g > 0:
                        y = y + red[at, :]
                    red[at, :] = y
                    if g == groups - 1:
                        carry = fold(carry, y)
                if g == groups - 1:
                    keep_sums(carry)

        for stage in range(stages):
            all_stats(first + stage, stat_send).wait()
        return 0

    lax.fori_loop(0, layers, layer_step, 0)


def finish(expanded, x, last, out_hbm, buffer, out_sem):
    chunks, count, mid = x.shape
    rows, width, chans = out_hbm.shape
    many = divisor(rows, FINAL_ROWS)

    def out_copy(row):
        at = pl.ds(row, many)
        return pltpu.make_async_copy(buffer.at[at], out_hbm.at[at], out_sem.at[row // many])

    for row in range(0, rows, many):
        at = pl.ds(row * width, many * width)
        for c in range(chunks):
            cols = slice(c * mid, (c + 1) * mid)
            y = expanded[c, at, :] * last[0:1, cols] + last[1:2, cols]
            y = jnp.maximum(y + x[c, at, :].astype(jnp.float32), 0.0)
            buffer[pl.ds(row, many), :, cols] = y.astype(jnp.bfloat16).reshape(many, width, mid)
        out_copy(row).start()
    for row in range(0, rows, many):
        out_copy(row).wait()


def solution(mesh):
    n = mesh.shape["slab"]

    def local(section_input, w_reduce, w_spatial, w_expand, gain_mid, shift_mid, gain_out, shift_out):
        rows, width, chans = section_input.shape
        layers, _, mid = w_reduce.shape
        chunks = chans // mid
        group = divisor(chunks, GROUP)
        count = rows * width
        stages = layers * (2 + chunks // group)
        wide = group * mid
        bf16, f32 = jnp.bfloat16, jnp.float32
        hbm = pl.BlockSpec(memory_space=pl.ANY)
        vmem = pl.BlockSpec(memory_space=pltpu.VMEM)
        held = pl.pallas_call(
            functools.partial(kernel, n),
            out_shape=[
                pltpu.VMEM((chunks, count, mid), f32),
                pltpu.VMEM((chunks, count, mid), bf16),
                pltpu.VMEM((2, chans), f32),
            ],
            in_specs=[hbm] * 4 + [vmem] * 4,
            out_specs=[vmem] * 3,
            scratch_shapes=[
                pltpu.VMEM(w_reduce.shape, bf16),
                pltpu.VMEM(w_spatial.shape, bf16),
                pltpu.VMEM(w_expand.shape, bf16),
                pltpu.VMEM((count, mid), f32),
                pltpu.VMEM(((rows + 2) * width, 3 * mid), bf16),
                pltpu.VMEM((count, mid), bf16),
                pltpu.VMEM((layers, 2, width, mid), bf16),
                pltpu.VMEM((layers, 2, width, mid), bf16),
                pltpu.VMEM((stages, 2, wide), f32),
                pltpu.VMEM((stages, n, 2, wide), f32),
                pltpu.VMEM((2, LANES, 8, mid), f32),
                pltpu.SemaphoreType.DMA((rows, chunks)),
                pltpu.SemaphoreType.DMA((3, layers)),
                pltpu.SemaphoreType.DMA((layers, 2)),
                pltpu.SemaphoreType.DMA((layers, 2)),
                pltpu.SemaphoreType.DMA((stages,)),
                pltpu.SemaphoreType.DMA((stages,)),
            ],
            compiler_params=pltpu.CompilerParams(
                collective_id=0, has_side_effects=True, vmem_limit_bytes=40 * 1024 * 1024
            ),
            name="blocks",
        )(section_input, w_reduce, w_spatial, w_expand, gain_mid, shift_mid, gain_out, shift_out)
        held = [pltpu.with_memory_space_constraint(a, pltpu.VMEM) for a in held]
        return pl.pallas_call(
            finish,
            out_shape=jax.ShapeDtypeStruct(section_input.shape, bf16),
            in_specs=[vmem] * 3,
            out_specs=hbm,
            scratch_shapes=[
                pltpu.VMEM((rows, width, chans), bf16),
                pltpu.SemaphoreType.DMA((rows // divisor(rows, FINAL_ROWS),)),
            ],
            compiler_params=pltpu.CompilerParams(vmem_limit_bytes=16 * 1024 * 1024),
            name="finish",
        )(*held)

    placed = (P(("img", "slab"), None, None), P(), P(), P(), P(), P(), P(), P())
    return jax.shard_map(
        local, mesh=mesh, in_specs=placed, out_specs=P(("img", "slab"), None, None), check_vma=False
    )
```

time: 76.2 us -> 69.8 us (0.916)
  Pallas kernels: 71.3 us -> 65.1 us
    pallas_call x1 -> x2, Pallas kernels: 71.3 us -> 65.1 us  [the longest x1 62.8 us: local(): pl.pallas_call(functools.partial(kernel, n), out_shape=[pltpu.VMEM((chunk...]
    unnamed x1 -> x10, local copies, waits for them, and re-layouts: 4.64 us -> 4.22 us
where the time goes in v1:
time: 69.8 us; the launch traced here: 69.4 us
  Pallas kernels  65.1 us (93%)
  local copies, waits for them, and re-layouts  4.22 us (6%)
    pallas_call x1, Pallas kernels, local(): pl.pallas_call(functools.partial(kernel, n), out_shape=[pltpu.VMEM((chunk...  62.8 us
    unnamed x10, local copies, waits for them, and re-layouts  4.22 us
    pallas_call x1, Pallas kernels, local(): pl.pallas_call(finish, out_shape=jax.ShapeDtypeStruct(section_input.shape...  2.35 us

profile of v1, /device:TPU:0, one launch (start us, length us, event | category | flops | bytes accessed | tf_op | source)
XLA Modules:
  0.0 69.4 jit_solution(7444297949266216747)
XLA Ops:
  0.0 0.0 copy-start
  0.0 1.4 %copy-done = bf16[3,1024,256]{2,1,0:T(8,128)(2,1)S(1)} copy-done((bf16[3,1024,256]{2,1,0:T(8,128)(2,1)S(1)}, bf16[3,1024,256]{2,1,0:T(8,128)(2,1)}, u32[]{:S(2)}) %copy-start) | copy-done | bytes 1572888
  1.4 0.0 copy-start.1
  1.4 0.7 %copy-done.1 = f32[3,1024]{1,0:T(4,128)S(1)} copy-done((f32[3,1024]{1,0:T(4,128)S(1)}, f32[3,1024]{1,0:T(4,128)}, u32[]{:S(2)}) %copy-start.1) | copy-done | bytes 12312
  2.1 0.0 copy-start.2
  2.1 0.7 %copy-done.2 = f32[3,1024]{1,0:T(4,128)S(1)} copy-done((f32[3,1024]{1,0:T(4,128)S(1)}, f32[3,1024]{1,0:T(4,128)}, u32[]{:S(2)}) %copy-start.2) | copy-done | bytes 12312
  2.8 0.0 copy-start.3
  2.8 0.7 copy-done.3
  3.5 0.0 copy-start.4
  3.5 0.7 copy-done.4
  4.2 62.8 %blocks.1 = (f32[4,2048,256]{2,1,0:T(8,128)S(1)}, bf16[4,2048,256]{2,1,0:T(8,128)(2,1)S(1)}, f32[2,1024]{1,0:T(2,128)S(1)}) custom-call(bf16[8,256,1024]{2,1,0:T(8,128)(2,1)} %x_hbm.1, bf16[3,1024,256]{2,1,0:T(8,128)(2,1)S(1)} %copy-done, bf16[3,9,256,256]{3,2,1,0:T(8,128)(2,1)} %ws_hbm.1, bf16[3,256,1024]{2,1,0:T(8,128)(2,1)} %we_hbm.1, ...), custom_call_target="tpu_custom_call" | custom-call | tf_op jit(solution)/shard_map/blocks/pallas_call | solution.py:346
  67.0 2.4 %finish.1 = bf16[8,256,1024]{2,1,0:T(8,128)(2,1)} custom-call(f32[4,2048,256]{2,1,0:T(8,128)S(1)} %get-tuple-element.8.expanded, bf16[4,2048,256]{2,1,0:T(8,128)(2,1)S(1)} %get-tuple-element.9.x, f32[2,1024]{1,0:T(2,128)S(1)} %get-tuple-element.10.last), custom_call_target="tpu_custom_call" | custom-call | tf_op jit(solution)/shard_map/finish/pallas_call | solution.py:380
Async XLA Ops:
  0.0 1.4 %copy-start = (bf16[3,1024,256]{2,1,0:T(8,128)(2,1)S(1)}, bf16[3,1024,256]{2,1,0:T(8,128)(2,1)}, u32[]{:S(2)}) copy-start(bf16[3,1024,256]{2,1,0:T(8,128)(2,1)} %wr_hbm.1) | copy-start | bytes 4718596
  1.4 0.7 %copy-start.1 = (f32[3,1024]{1,0:T(4,128)S(1)}, f32[3,1024]{1,0:T(4,128)}, u32[]{:S(2)}) copy-start(f32[3,1024]{1,0:T(4,128)} %gain_out.1) | copy-start | bytes 36868
  2.1 0.7 %copy-start.2 = (f32[3,1024]{1,0:T(4,128)S(1)}, f32[3,1024]{1,0:T(4,128)}, u32[]{:S(2)}) copy-start(f32[3,1024]{1,0:T(4,128)} %shift_out.1) | copy-start | bytes 36868
  2.8 0.7 copy-start.3
  3.5 0.7 copy-start.4

commit v2 on v1

--- a/solution.py
+++ b/solution.py
@@ -13,8 +13,7 @@
 CONV_ROWS = 2
 EXPAND_ROWS = 1
 OUTPUT_ROWS = 1
-FINAL_ROWS = 1
-LANES = 8
+LANES = 2
 GROUP = 2
 
 
@@ -23,13 +22,13 @@
 
 
 def kernel(
-    n, x_hbm, wr_hbm, ws_hbm, we_hbm, gain_mid, shift_mid, gain_out, shift_out,
+    n, x_hbm, wr_hbm, ws_hbm, we_hbm, gain_mid_hbm, shift_mid_hbm, gain_out_hbm, shift_out_hbm,
     expanded, x, last,
-    wr, ws, we, red, taps, inner, halo_out, halo_in, stat_out, stat, sums,
-    x_sem, w_sem, halo_send, halo_recv, stat_send, stat_recv,
+    gain_mid, shift_mid, gain_out, shift_out, wr, ws, we, red, taps, inner, halo_out, halo_in, stat_out, stat, sums,
+    g_sem, x_sem, w_sem, halo_send, halo_recv, stat_send, stat_recv,
 ):
-    chunks, count, mid = x.shape
-    rows, width, chans = x_hbm.shape
+    chunks, rows, width, mid = x.shape
+    count = rows * width
     layers = wr.shape[0]
     group = divisor(chunks, GROUP)
     groups = chunks // group
@@ -48,36 +47,54 @@
 
     def weight_copy(kind, layer):
         source, target = ((wr_hbm, wr), (ws_hbm, ws), (we_hbm, we))[kind]
-        return pltpu.make_async_copy(source.at[layer], target.at[layer], w_sem.at[kind, layer])
-
-    def x_copy(row, c):
+        return pltpu.make_async_copy(source.at[layer], target.at[layer], w_sem.at[kind])
+
+    reduce_rows = divisor(rows, REDUCE_ROWS)
+
+    def x_copy(step, c):
+        at = pl.ds(step * reduce_rows, reduce_rows)
         return pltpu.make_async_copy(
-            x_hbm.at[row, :, pl.ds(c * mid, mid)],
-            x.at[c, pl.ds(row * width, width), :],
-            x_sem.at[row, c],
-        )
-
+            x_hbm.at[at, :, pl.ds(c * mid, mid)], x.at[c, at], x_sem.at[step]
+        )
+
+    def x_arrival(step):
+        whole = x.at[:, pl.ds(step * reduce_rows, reduce_rows)]
+        return pltpu.make_async_copy(whole, whole, x_sem.at[step])
+
+    small = [
+        pltpu.make_async_copy(source, target, g_sem.at[i])
+        for i, (source, target) in enumerate(
+            (
+                (gain_mid_hbm, gain_mid),
+                (shift_mid_hbm, shift_mid),
+                (gain_out_hbm, gain_out),
+                (shift_out_hbm, shift_out),
+            )
+        )
+    ]
     weight_copy(0, 0).start()
-    for row in range(rows):
+    for step in range(rows // reduce_rows):
         for c in range(chunks):
-            x_copy(row, c).start()
+            x_copy(step, c).start()
+    for copy in small:
+        copy.start()
 
     def span(row, many=1):
         return pl.ds(row * width, many * width)
 
-    def stat_copy(stage, cols, k):
+    def stat_copy(stage, kind, k):
         return pltpu.make_async_remote_copy(
             src_ref=stat_out.at[stage],
             dst_ref=stat.at[stage, k],
-            send_sem=stat_send.at[stage],
-            recv_sem=stat_recv.at[stage],
+            send_sem=stat_send.at[kind],
+            recv_sem=stat_recv.at[kind],
             device_id={"slab": peer(k)},
             device_id_type=MESH,
         )
 
-    def all_stats(stage, sem):
+    def all_stats(stage, kind, sem):
         others = stat.at[stage, pl.ds(1, n - 1)]
-        return pltpu.make_async_copy(others, others, sem.at[stage])
+        return pltpu.make_async_copy(others, others, sem.at[kind])
 
     def fold(carry, y):
         y = y.reshape(-1, LANES, 8, y.shape[-1])
@@ -87,21 +104,25 @@
         zero = jnp.zeros((LANES, 8, cols), jnp.float32)
         return zero, zero
 
+    order = sorted(range(1, n), key=lambda k: (1 - k % 2, -abs(2 * k - n)))
+
     def total(part):
         return jnp.sum(jnp.sum(part, axis=0), axis=0, keepdims=True)
 
-    def send_stats(stage, carry):
+    def send_stats(layer, kind, carry):
+        stage = layer * stages + kind
         first = total(carry[0])
         both = jnp.concatenate([first, total(carry[1])], axis=0)
         cols = both.shape[-1]
         stat_out[stage, :, 0:cols] = both
         stat[stage, 0, :, 0:cols] = both
-        for k in range(1, n):
-            stat_copy(stage, cols, k).start()
+        for k in order:
+            stat_copy(stage, kind, k).start()
         return first
 
-    def affine(stage, gain, shift):
-        all_stats(stage, stat_recv).wait()
+    def affine(layer, kind, gain, shift):
+        stage = layer * stages + kind
+        all_stats(stage, kind, stat_recv).wait()
         cols = gain.shape[-1]
         both = jnp.sum(stat[stage], axis=0)[:, 0:cols]
         mean = both[0:1] * inv_count
@@ -113,8 +134,8 @@
         return pltpu.make_async_remote_copy(
             src_ref=halo_out.at[layer, side],
             dst_ref=halo_in.at[layer, 1 - side],
-            send_sem=halo_send.at[layer, side],
-            recv_sem=halo_recv.at[layer, 1 - side],
+            send_sem=halo_send.at[side],
+            recv_sem=halo_recv.at[1 - side],
             device_id={"slab": peer(n - 1 if side == 0 else 1)},
             device_id_type=MESH,
         )
@@ -123,8 +144,8 @@
         return pltpu.make_async_remote_copy(
             src_ref=halo_out.at[layer, side],
             dst_ref=halo_in.at[layer, side],
-            send_sem=halo_send.at[layer, side],
-            recv_sem=halo_recv.at[layer, side],
+            send_sem=halo_send.at[side],
+            recv_sem=halo_recv.at[side],
             device_id={"slab": peer(n - 1 if side == 0 else 1)},
             device_id_type=MESH,
         )
@@ -156,26 +177,25 @@
 
     weight_copy(0, 0).wait()
     carry = zeros(mid)
-    reduce_rows = divisor(rows, REDUCE_ROWS)
     for row in range(0, rows, reduce_rows):
-        for r in range(row, row + reduce_rows):
-            for c in range(chunks):
-                x_copy(r, c).wait()
+        x_arrival(row // reduce_rows).wait()
         for r in range(row, row + reduce_rows):
             y = jnp.dot(
-                jnp.concatenate([x[c, span(r), :] for c in range(chunks)], axis=1),
+                jnp.concatenate([x[c, r] for c in range(chunks)], axis=1),
                 wr[0],
                 preferred_element_type=jnp.float32,
             )
             red[span(r), :] = y
             carry = fold(carry, y)
     keep_sums(carry)
+    for copy in small:
+        copy.wait()
     pl.semaphore_wait(barrier, n - 1)
 
     def layer_step(layer, _):
         first = layer * stages
 
-        local_mean = send_stats(first, (sums[0], sums[1])) * inv_local
+        local_mean = send_stats(layer, 0, (sums[0], sums[1])) * inv_local
         for side in range(2):
             row = 0 if side == 0 else rows - 1
             halo_out[layer, side] = (red[span(row), :] - local_mean).astype(jnp.bfloat16)
@@ -192,7 +212,7 @@
             weight_copy(0, layer + 1).start()
 
         weight_copy(1, layer).wait()
-        scale, shift = affine(first, gain_mid[layer, 0:1], shift_mid[layer, 0:1])
+        scale, shift = affine(layer, 0, gain_mid[layer, 0:1], shift_mid[layer, 0:1])
 
         def hidden(row):
             store_taps(row + 1, jnp.maximum(red[span(row), :] * scale + shift, 0.0))
@@ -229,10 +249,10 @@
 
         for row in (0, rows - 1):
             carry = fold(carry, conv(row, 1))
-        send_stats(first + 1, carry)
+        send_stats(layer, 1, carry)
 
         weight_copy(2, layer).wait()
-        scale, shift = affine(first + 1, gain_mid[layer, 1:2], shift_mid[layer, 1:2])
+        scale, shift = affine(layer, 1, gain_mid[layer, 1:2], shift_mid[layer, 1:2])
 
         expand_rows = divisor(rows, EXPAND_ROWS)
         for g in range(groups):
@@ -253,7 +273,8 @@
                     expanded[c, at, :] = y
                     parts[i] = fold(parts[i], y)
             send_stats(
-                first + 2 + g,
+                layer,
+                2 + g,
                 tuple(jnp.concatenate([p[j] for p in parts], axis=-1) for j in range(2)),
             )
 
@@ -266,7 +287,7 @@
         for g in range(groups):
             cols = slice(g * wide, (g + 1) * wide)
             scale, shift = affine(
-                first + 2 + g, gain_out[pl.ds(layer, 1), cols], shift_out[pl.ds(layer, 1), cols]
+                layer, 2 + g, gain_out[pl.ds(layer, 1), cols], shift_out[pl.ds(layer, 1), cols]
             )
 
             @pl.when(layer == layers - 1)
@@ -284,9 +305,8 @@
                         c = g * group + i
                         part = slice(i * mid, (i + 1) * mid)
                         y = expanded[c, at, :] * scale[:, part] + shift[:, part]
-                        y = y + x[c, at, :].astype(jnp.float32)
-                        y = jnp.maximum(y, 0.0).astype(jnp.bfloat16)
-                        x[c, at, :] = y
+                        y = jnp.maximum(y.astype(jnp.bfloat16) + x[c, row], 0.0)
+                        x[c, row] = y
                         blocks.append(y)
                     y = jnp.dot(
                         jnp.concatenate(blocks, axis=1),
@@ -302,30 +322,26 @@
                     keep_sums(carry)
 
         for stage in range(stages):
-            all_stats(first + stage, stat_send).wait()
+            all_stats(first + stage, stage, stat_send).wait()
         return 0
 
     lax.fori_loop(0, layers, layer_step, 0)
 
 
 def finish(expanded, x, last, out_hbm, buffer, out_sem):
-    chunks, count, mid = x.shape
-    rows, width, chans = out_hbm.shape
-    many = divisor(rows, FINAL_ROWS)
+    chunks, rows, width, mid = x.shape
 
     def out_copy(row):
-        at = pl.ds(row, many)
-        return pltpu.make_async_copy(buffer.at[at], out_hbm.at[at], out_sem.at[row // many])
-
-    for row in range(0, rows, many):
-        at = pl.ds(row * width, many * width)
+        return pltpu.make_async_copy(buffer.at[row], out_hbm.at[row], out_sem.at[row])
+
+    for row in range(rows):
+        at = pl.ds(row * width, width)
         for c in range(chunks):
             cols = slice(c * mid, (c + 1) * mid)
             y = expanded[c, at, :] * last[0:1, cols] + last[1:2, cols]
-            y = jnp.maximum(y + x[c, at, :].astype(jnp.float32), 0.0)
-            buffer[pl.ds(row, many), :, cols] = y.astype(jnp.bfloat16).reshape(many, width, mid)
+            buffer[row, :, cols] = jnp.maximum(y.astype(jnp.bfloat16) + x[c, row], 0.0)
         out_copy(row).start()
-    for row in range(0, rows, many):
+    for row in range(rows):
         out_copy(row).wait()
 
 
@@ -347,12 +363,16 @@
             functools.partial(kernel, n),
             out_shape=[
                 pltpu.VMEM((chunks, count, mid), f32),
-                pltpu.VMEM((chunks, count, mid), bf16),
+                pltpu.VMEM((chunks, rows, width, mid), bf16),
                 pltpu.VMEM((2, chans), f32),
             ],
-            in_specs=[hbm] * 4 + [vmem] * 4,
+            in_specs=[hbm] * 8,
             out_specs=[vmem] * 3,
             scratch_shapes=[
+                pltpu.VMEM(gain_mid.shape, f32),
+                pltpu.VMEM(shift_mid.shape, f32),
+                pltpu.VMEM(gain_out.shape, f32),
+                pltpu.VMEM(shift_out.shape, f32),
                 pltpu.VMEM(w_reduce.shape, bf16),
                 pltpu.VMEM(w_spatial.shape, bf16),
                 pltpu.VMEM(w_expand.shape, bf16),
@@ -364,18 +384,27 @@
                 pltpu.VMEM((stages, 2, wide), f32),
                 pltpu.VMEM((stages, n, 2, wide), f32),
                 pltpu.VMEM((2, LANES, 8, mid), f32),
-                pltpu.SemaphoreType.DMA((rows, chunks)),
-                pltpu.SemaphoreType.DMA((3, layers)),
-                pltpu.SemaphoreType.DMA((layers, 2)),
-                pltpu.SemaphoreType.DMA((layers, 2)),
-                pltpu.SemaphoreType.DMA((stages,)),
-                pltpu.SemaphoreType.DMA((stages,)),
+                pltpu.SemaphoreType.DMA((4,)),
+                pltpu.SemaphoreType.DMA((rows // divisor(rows, REDUCE_ROWS),)),
+                pltpu.SemaphoreType.DMA((3,)),
+                pltpu.SemaphoreType.DMA((2,)),
+                pltpu.SemaphoreType.DMA((2,)),
+                pltpu.SemaphoreType.DMA((stages // layers,)),
+                pltpu.SemaphoreType.DMA((stages // layers,)),
             ],
             compiler_params=pltpu.CompilerParams(
                 collective_id=0, has_side_effects=True, vmem_limit_bytes=40 * 1024 * 1024
             ),
             name="blocks",
-        )(section_input, w_reduce, w_spatial, w_expand, gain_mid, shift_mid, gain_out, shift_out)
+        )(
+            *(
+                pltpu.with_memory_space_constraint(a, pltpu.HBM)
+                for a in (
+                    section_input, w_reduce, w_spatial, w_expand,
+                    gain_mid, shift_mid, gain_out, shift_out,
+                )
+            )
+        )
         held = [pltpu.with_memory_space_constraint(a, pltpu.VMEM) for a in held]
         return pl.pallas_call(
             finish,
@@ -384,7 +413,7 @@
             out_specs=hbm,
             scratch_shapes=[
                 pltpu.VMEM((rows, width, chans), bf16),
-                pltpu.SemaphoreType.DMA((rows // divisor(rows, FINAL_ROWS),)),
+                pltpu.SemaphoreType.DMA((rows,)),
             ],
             compiler_params=pltpu.CompilerParams(vmem_limit_bytes=16 * 1024 * 1024),
             name="finish",

time: 69.8 us -> 64.2 us (0.920)
  local copies, waits for them, and re-layouts: 4.22 us -> 0 us
  Pallas kernels: 65.1 us -> 64 us
    unnamed x10 -> x0, local copies, waits for them, and re-layouts: 4.22 us -> none
    pallas_call x1, Pallas kernels: 62.8 us -> 61.8 us  [local(): pl.pallas_call(functools.partial(kernel, n), out_shape=[pltpu.VMEM((chunk...]
where the time goes in v2:
time: 64.2 us; the launch traced here: 64 us
  Pallas kernels  64 us (100%)
    pallas_call x1, Pallas kernels, local(): pl.pallas_call(functools.partial(kernel, n), out_shape=[pltpu.VMEM((chunk...  61.8 us
    pallas_call x1, Pallas kernels, local(): pl.pallas_call(finish, out_shape=jax.ShapeDtypeStruct(section_input.shape...  2.22 us

profile of v2, /device:TPU:0, one launch (start us, length us, event | category | flops | bytes accessed | tf_op | source)
XLA Modules:
  0.0 64.0 jit_solution(2188294493275609560)
XLA Ops:
  0.0 61.8 %blocks.1 = (f32[4,2048,256]{2,1,0:T(8,128)S(1)}, bf16[4,8,256,256]{3,2,1,0:T(8,128)(2,1)S(1)}, f32[2,1024]{1,0:T(2,128)S(1)}) custom-call(bf16[8,256,1024]{2,1,0:T(8,128)(2,1)} %x_hbm.1, bf16[3,1024,256]{2,1,0:T(8,128)(2,1)} %wr_hbm.1, bf16[3,9,256,256]{3,2,1,0:T(8,128)(2,1)} %ws_hbm.1, bf16[3,256,1024]{2,1,0:T(8,128)(2,1)} %we_hbm.1, ...), custom_call_target="tpu_custom_call" | custom-call | tf_op jit(solution)/shard_map/blocks/pallas_call | solution.py:362
  61.8 2.2 %finish.1 = bf16[8,256,1024]{2,1,0:T(8,128)(2,1)} custom-call(f32[4,2048,256]{2,1,0:T(8,128)S(1)} %get-tuple-element.8.expanded, bf16[4,8,256,256]{3,2,1,0:T(8,128)(2,1)S(1)} %get-tuple-element.9.x, f32[2,1024]{1,0:T(2,128)S(1)} %get-tuple-element.10.last), custom_call_target="tpu_custom_call" | custom-call | tf_op jit(solution)/shard_map/finish/pallas_call | solution.py:409

commit v3 on v2

--- a/solution.py
+++ b/solution.py
@@ -12,7 +12,6 @@
 REDUCE_ROWS = 2
 CONV_ROWS = 2
 EXPAND_ROWS = 1
-OUTPUT_ROWS = 1
 LANES = 2
 GROUP = 2
 
@@ -46,20 +45,29 @@
         pl.semaphore_signal(barrier, inc=1, device_id={"slab": peer(k)}, device_id_type=MESH)
 
     def weight_copy(kind, layer):
-        source, target = ((wr_hbm, wr), (ws_hbm, ws), (we_hbm, we))[kind]
+        source, target = ((wr_hbm, wr), (ws_hbm, ws))[kind]
         return pltpu.make_async_copy(source.at[layer], target.at[layer], w_sem.at[kind])
 
+    def expand_copy(layer, c):
+        return pltpu.make_async_copy(
+            we_hbm.at[layer, :, pl.ds(c * mid, mid)], we.at[layer, c], w_sem.at[2]
+        )
+
+    def expand_arrival(layer):
+        return pltpu.make_async_copy(we.at[layer], we.at[layer], w_sem.at[2])
+
     reduce_rows = divisor(rows, REDUCE_ROWS)
 
-    def x_copy(step, c):
-        at = pl.ds(step * reduce_rows, reduce_rows)
+    def x_copy(step, c, pick):
         return pltpu.make_async_copy(
-            x_hbm.at[at, :, pl.ds(c * mid, mid)], x.at[c, at], x_sem.at[step]
+            x_hbm.at[pick, :, pl.ds(c * mid, mid)], x.at[c, pick], x_sem.at[step]
         )
 
     def x_arrival(step):
         whole = x.at[:, pl.ds(step * reduce_rows, reduce_rows)]
         return pltpu.make_async_copy(whole, whole, x_sem.at[step])
+
+    steps = [list(range(i, i + reduce_rows)) for i in range(0, rows, reduce_rows)]
 
     small = [
         pltpu.make_async_copy(source, target, g_sem.at[i])
@@ -73,9 +81,9 @@
         )
     ]
     weight_copy(0, 0).start()
-    for step in range(rows // reduce_rows):
+    for step, picks in enumerate(steps):
         for c in range(chunks):
-            x_copy(step, c).start()
+            x_copy(step, c, pl.ds(picks[0], reduce_rows)).start()
     for copy in small:
         copy.start()
 
@@ -172,14 +180,17 @@
         sums[1] = carry[1]
 
     for side in range(2):
-        row = 0 if side == 0 else rows + 1
-        taps[span(row), :] = jnp.zeros((width, 3 * mid), jnp.bfloat16)
+
+        @pl.when(jnp.logical_not(has_neighbour(side)))
+        def _():
+            for layer in range(layers):
+                halo_in[layer, side] = jnp.zeros((width, mid), jnp.bfloat16)
 
     weight_copy(0, 0).wait()
     carry = zeros(mid)
-    for row in range(0, rows, reduce_rows):
-        x_arrival(row // reduce_rows).wait()
-        for r in range(row, row + reduce_rows):
+    for step, picks in enumerate(steps):
+        x_arrival(step).wait()
+        for r in picks:
             y = jnp.dot(
                 jnp.concatenate([x[c, r] for c in range(chunks)], axis=1),
                 wr[0],
@@ -205,7 +216,8 @@
                 halo_copy(layer, side).start()
 
         weight_copy(1, layer).start()
-        weight_copy(2, layer).start()
+        for c in range(chunks):
+            expand_copy(layer, c).start()
 
         @pl.when(layer < layers - 1)
         def _():
@@ -225,6 +237,14 @@
             )
             red[span(row, many), :] = y
             return y
+
+        def conv_edge(side, first, many):
+            row = 0 if side == 0 else rows - 1
+            return jnp.dot(
+                jnp.concatenate([taps[span(row + first + i), :] for i in range(many)], axis=1),
+                ws[layer, pl.ds(3 * first, 3 * many)].reshape(3 * many * mid, mid),
+                preferred_element_type=jnp.float32,
+            )
 
         carry = zeros(mid)
         done = 0
@@ -235,23 +255,32 @@
                 done += 1
             for r in range(row, row + conv_rows):
                 carry = fold(carry, conv(r, 1))
-
         for side in range(2):
-            row = 0 if side == 0 else rows + 1
+            red[span(0 if side == 0 else rows - 1), :] = conv_edge(side, 1 - side, 2)
+
+        for side in range(2):
 
             @pl.when(has_neighbour(side))
             def _():
                 halo_copy(layer, side).wait_send()
                 halo_arrival(layer, side).wait_recv()
-                theirs = stat[first, 1 if side == 0 else n - 1, 0:1, 0:mid] * inv_local
-                y = halo_in[layer, side].astype(jnp.float32) + theirs
-                store_taps(row, jnp.maximum(y * scale + shift, 0.0))
-
-        for row in (0, rows - 1):
-            carry = fold(carry, conv(row, 1))
+
+        for side in range(2):
+            row = 0 if side == 0 else rows + 1
+            there = jnp.where(has_neighbour(side), 1.0, 0.0)
+            y = halo_in[layer, side].astype(jnp.float32) * (scale * there)
+            theirs = stat[first, 1 if side == 0 else n - 1, 0:1, 0:mid] * inv_local
+            moved = theirs * scale + shift
+            store_taps(row, jnp.maximum(y + moved * there, 0.0))
+
+        for side in range(2):
+            at = span(0 if side == 0 else rows - 1)
+            y = conv_edge(side, 2 * side, 1) + red[at, :]
+            red[at, :] = y
+            carry = fold(carry, y)
         send_stats(layer, 1, carry)
 
-        weight_copy(2, layer).wait()
+        expand_arrival(layer).wait()
         scale, shift = affine(layer, 1, gain_mid[layer, 1:2], shift_mid[layer, 1:2])
 
         expand_rows = divisor(rows, EXPAND_ROWS)
@@ -267,7 +296,7 @@
                 for i in range(group):
                     c = g * group + i
                     y = jnp.dot(
-                        block, we[layer, :, c * mid : (c + 1) * mid],
+                        block, we[layer, c],
                         preferred_element_type=jnp.float32,
                     )
                     expanded[c, at, :] = y
@@ -282,7 +311,6 @@
         def _():
             weight_copy(0, layer + 1).wait()
 
-        output_rows = divisor(rows, OUTPUT_ROWS)
         carry = zeros(mid)
         for g in range(groups):
             cols = slice(g * wide, (g + 1) * wide)
@@ -298,8 +326,8 @@
             @pl.when(layer < layers - 1)
             def _():
                 carry = zeros(mid)
-                for row in range(0, rows, output_rows):
-                    at = span(row, output_rows)
+                for row in range(rows):
+                    at = span(row)
                     blocks = []
                     for i in range(group):
                         c = g * group + i
@@ -375,7 +403,7 @@
                 pltpu.VMEM(shift_out.shape, f32),
                 pltpu.VMEM(w_reduce.shape, bf16),
                 pltpu.VMEM(w_spatial.shape, bf16),
-                pltpu.VMEM(w_expand.shape, bf16),
+                pltpu.VMEM((layers, chunks, mid, mid), bf16),
                 pltpu.VMEM((count, mid), f32),
                 pltpu.VMEM(((rows + 2) * width, 3 * mid), bf16),
                 pltpu.VMEM((count, mid), bf16),

time: 64.2 us -> 62.7 us (0.977)
  Pallas kernels: 64 us -> 62.5 us
    pallas_call x1, Pallas kernels: 61.8 us -> 60.3 us  [local(): pl.pallas_call(functools.partial(kernel, n), out_shape=[pltpu.VMEM((chunk...]
where the time goes in v3:
time: 62.7 us; the launch traced here: 62.5 us
  Pallas kernels  62.5 us (100%)
    pallas_call x1, Pallas kernels, local(): pl.pallas_call(functools.partial(kernel, n), out_shape=[pltpu.VMEM((chunk...  60.3 us
    pallas_call x1, Pallas kernels, local(): pl.pallas_call(finish, out_shape=jax.ShapeDtypeStruct(section_input.shape...  2.22 us

profile of v3, /device:TPU:0, one launch (start us, length us, event | category | flops | bytes accessed | tf_op | source)
XLA Modules:
  0.0 62.5 jit_solution(4820146600178959643)
XLA Ops:
  0.0 60.3 %blocks.1 = (f32[4,2048,256]{2,1,0:T(8,128)S(1)}, bf16[4,8,256,256]{3,2,1,0:T(8,128)(2,1)S(1)}, f32[2,1024]{1,0:T(2,128)S(1)}) custom-call(bf16[8,256,1024]{2,1,0:T(8,128)(2,1)} %x_hbm.1, bf16[3,1024,256]{2,1,0:T(8,128)(2,1)} %wr_hbm.1, bf16[3,9,256,256]{3,2,1,0:T(8,128)(2,1)} %ws_hbm.1, bf16[3,256,1024]{2,1,0:T(8,128)(2,1)} %we_hbm.1, ...), custom_call_target="tpu_custom_call" | custom-call | tf_op jit(solution)/shard_map/blocks/pallas_call | solution.py:390
  60.3 2.2 %finish.1 = bf16[8,256,1024]{2,1,0:T(8,128)(2,1)} custom-call(f32[4,2048,256]{2,1,0:T(8,128)S(1)} %get-tuple-element.8.expanded, bf16[4,8,256,256]{3,2,1,0:T(8,128)(2,1)S(1)} %get-tuple-element.9.x, f32[2,1024]{1,0:T(2,128)S(1)} %get-tuple-element.10.last), custom_call_target="tpu_custom_call" | custom-call | tf_op jit(solution)/shard_map/finish/pallas_call | solution.py:437

commit v4 on v3

--- a/solution.py
+++ b/solution.py
@@ -13,7 +13,7 @@
 CONV_ROWS = 2
 EXPAND_ROWS = 1
 LANES = 2
-GROUP = 2
+GROUP = 1
 
 
 def divisor(rows, most):
@@ -40,10 +40,6 @@
     def peer(k):
         return lax.rem(me + k, n)
 
-    barrier = pltpu.get_barrier_semaphore()
-    for k in range(1, n):
-        pl.semaphore_signal(barrier, inc=1, device_id={"slab": peer(k)}, device_id_type=MESH)
-
     def weight_copy(kind, layer):
         source, target = ((wr_hbm, wr), (ws_hbm, ws))[kind]
         return pltpu.make_async_copy(source.at[layer], target.at[layer], w_sem.at[kind])
@@ -64,10 +60,12 @@
         )
 
     def x_arrival(step):
-        whole = x.at[:, pl.ds(step * reduce_rows, reduce_rows)]
+        whole = x.at[:, pl.ds(steps[step][0], len(steps[step]))]
         return pltpu.make_async_copy(whole, whole, x_sem.at[step])
 
     steps = [list(range(i, i + reduce_rows)) for i in range(0, rows, reduce_rows)]
+    if len(steps) > 1:
+        steps = steps[:-2] + [steps[-2] + steps[-1]]
 
     small = [
         pltpu.make_async_copy(source, target, g_sem.at[i])
@@ -83,9 +81,13 @@
     weight_copy(0, 0).start()
     for step, picks in enumerate(steps):
         for c in range(chunks):
-            x_copy(step, c, pl.ds(picks[0], reduce_rows)).start()
+            x_copy(step, c, pl.ds(picks[0], len(picks))).start()
     for copy in small:
         copy.start()
+
+    barrier = pltpu.get_barrier_semaphore()
+    for k in range(1, n):
+        pl.semaphore_signal(barrier, inc=1, device_id={"slab": peer(k)}, device_id_type=MESH)
 
     def span(row, many=1):
         return pl.ds(row * width, many * width)
@@ -320,8 +322,15 @@
 
             @pl.when(layer == layers - 1)
             def _():
-                last[0:1, cols] = scale
-                last[1:2, cols] = shift
+                if g == groups - 1:
+                    last[0:1, :] = scale
+                    last[1:2, :] = shift
+                else:
+                    for row in range(rows):
+                        for c in range(g * group, (g + 1) * group):
+                            part = slice((c - g * group) * mid, (c - g * group + 1) * mid)
+                            y = expanded[c, span(row), :] * scale[:, part] + shift[:, part]
+                            x[c, row] = jnp.maximum(y.astype(jnp.bfloat16) + x[c, row], 0.0)
 
             @pl.when(layer < layers - 1)
             def _():
@@ -359,18 +368,31 @@
 def finish(expanded, x, last, out_hbm, buffer, out_sem):
     chunks, rows, width, mid = x.shape
 
-    def out_copy(row):
-        return pltpu.make_async_copy(buffer.at[row], out_hbm.at[row], out_sem.at[row])
-
+    done = chunks - last.shape[1] // mid
+
+    def out_copy(c):
+        cols = pl.ds(c * mid, mid)
+        return pltpu.make_async_copy(x.at[c], out_hbm.at[:, :, cols], out_sem.at[c])
+
+    def row_copy(row):
+        cols = pl.ds(done * mid, (chunks - done) * mid)
+        return pltpu.make_async_copy(
+            buffer.at[row], out_hbm.at[row, :, cols], out_sem.at[done + row]
+        )
+
+    for c in range(done):
+        out_copy(c).start()
     for row in range(rows):
         at = pl.ds(row * width, width)
-        for c in range(chunks):
-            cols = slice(c * mid, (c + 1) * mid)
+        for c in range(done, chunks):
+            cols = slice((c - done) * mid, (c - done + 1) * mid)
             y = expanded[c, at, :] * last[0:1, cols] + last[1:2, cols]
             buffer[row, :, cols] = jnp.maximum(y.astype(jnp.bfloat16) + x[c, row], 0.0)
-        out_copy(row).start()
+        row_copy(row).start()
+    for c in range(done):
+        out_copy(c).wait()
     for row in range(rows):
-        out_copy(row).wait()
+        row_copy(row).wait()
 
 
 def solution(mesh):
@@ -392,7 +414,7 @@
             out_shape=[
                 pltpu.VMEM((chunks, count, mid), f32),
                 pltpu.VMEM((chunks, rows, width, mid), bf16),
-                pltpu.VMEM((2, chans), f32),
+                pltpu.VMEM((2, wide), f32),
             ],
             in_specs=[hbm] * 8,
             out_specs=[vmem] * 3,
@@ -413,7 +435,7 @@
                 pltpu.VMEM((stages, n, 2, wide), f32),
                 pltpu.VMEM((2, LANES, 8, mid), f32),
                 pltpu.SemaphoreType.DMA((4,)),
-                pltpu.SemaphoreType.DMA((rows // divisor(rows, REDUCE_ROWS),)),
+                pltpu.SemaphoreType.DMA((max(1, rows // divisor(rows, REDUCE_ROWS) - 1),)),
                 pltpu.SemaphoreType.DMA((3,)),
                 pltpu.SemaphoreType.DMA((2,)),
                 pltpu.SemaphoreType.DMA((2,)),
@@ -440,8 +462,8 @@
             in_specs=[vmem] * 3,
             out_specs=hbm,
             scratch_shapes=[
-                pltpu.VMEM((rows, width, chans), bf16),
-                pltpu.SemaphoreType.DMA((rows,)),
+                pltpu.VMEM((rows, width, wide), bf16),
+                pltpu.SemaphoreType.DMA((chunks + rows,)),
             ],
             compiler_params=pltpu.CompilerParams(vmem_limit_bytes=16 * 1024 * 1024),
             name="finish",

time: 62.7 us -> 62.3 us (level)
  no operation moved by 1% of the time
where the time goes in v4:
time: 62.3 us; the launch traced here: 62.1 us
  Pallas kernels  62 us (100%)
    pallas_call x1, Pallas kernels, local(): pl.pallas_call(functools.partial(kernel, n), out_shape=[pltpu.VMEM((chunk...  60 us
    pallas_call x1, Pallas kernels, local(): pl.pallas_call(finish, out_shape=jax.ShapeDtypeStruct(section_input.shape...  2.1 us

profile of v4, /device:TPU:0, one launch (start us, length us, event | category | flops | bytes accessed | tf_op | source)
XLA Modules:
  0.0 62.1 jit_solution(3224559630991913326)
XLA Ops:
  0.0 60.0 %blocks.1 = (f32[4,2048,256]{2,1,0:T(8,128)S(1)}, bf16[4,8,256,256]{3,2,1,0:T(8,128)(2,1)S(1)}, f32[2,256]{1,0:T(2,128)S(1)}) custom-call(bf16[8,256,1024]{2,1,0:T(8,128)(2,1)} %x_hbm.1, bf16[3,1024,256]{2,1,0:T(8,128)(2,1)} %wr_hbm.1, bf16[3,9,256,256]{3,2,1,0:T(8,128)(2,1)} %ws_hbm.1, bf16[3,256,1024]{2,1,0:T(8,128)(2,1)} %we_hbm.1, ...), custom_call_target="tpu_custom_call" | custom-call | tf_op jit(solution)/shard_map/blocks/pallas_call | solution.py:412
  60.0 2.1 %finish.1 = bf16[8,256,1024]{2,1,0:T(8,128)(2,1)} custom-call(f32[4,2048,256]{2,1,0:T(8,128)S(1)} %get-tuple-element.8.expanded, bf16[4,8,256,256]{3,2,1,0:T(8,128)(2,1)S(1)} %get-tuple-element.9.x, f32[2,256]{1,0:T(2,128)S(1)} %get-tuple-element.10.last), custom_call_target="tpu_custom_call" | custom-call | tf_op jit(solution)/shard_map/finish/pallas_call | solution.py:459
